TPU v7x, 32 devices: a whole 2x2x4 slice. The times are simulated.
32 devices in a mesh: blk: 4 (over y, x), in: 8 (over z, core).
Axes of the slice: x: 2, y: 2, z: 4, core: 2. Of those that a mesh axis runs over, the one named last changes fastest.
Arguments:
- heat_source: float32 [6144, 2048], P('blk', 'in'), may hold values from -6 to 6
- conductance: float32 [6144, 2048], P('blk', 'in'), may hold values from 0.1 to 2
- start_field: float32 [6144, 2048], P('blk', 'in'), may hold values from -6 to 8
- colour_map: int32 [2, 4], P(None, 'blk'), may hold values from 0 to 1
- projection: int32 [4, 2, 2048], P('blk', None, 'in'), may hold values from 0 to 2047
- face_counts: int32 [4, 2], P('blk'), may hold values from 1024 to 2048
Outputs:
- temperature: float32 [6144, 2048], P('blk', 'in')
- block_rms: float32 [4], P('blk')
Inputs may be any that keep to these rules, and one draw needn't show every extreme that they name: `colour_map`: neighbouring blocks may share a colour.
All inputs are finite; a program needn't handle non-finite values.
Results may differ from a plain program's by a relative error of at most 0.00002.
Values sent between devices are 32-bit elements; how exact they have to be, the bound alone decides.
A program may use at most 64 MiB of HBM per device.

v0:
```python
import functools

import jax
import jax.numpy as jnp
from jax import lax
from jax.experimental import pallas as pl
from jax.experimental.pallas import tpu as pltpu
from jax.sharding import PartitionSpec as P

SWEEPS = 2
INNER = 4
LANES = 128
SUB = 8
WINDOW = 16
STRIP = 32
CHUNK = 64
MESH = pl.DeviceIdType.MESH
F32 = jnp.float32


def shift_lanes(tiles, lane):
    n = len(tiles)
    fwd = [pltpu.roll(x, 1, 1) for x in tiles]
    back = [pltpu.roll(x, LANES - 1, 1) for x in tiles]
    left = [jnp.where(lane == 0, fwd[(t - 1) % n], fwd[t]) for t in range(n)]
    right = [jnp.where(lane == LANES - 1, back[(t + 1) % n], back[t]) for t in range(n)]
    return left, right


def kernel(
    nblk, nin, colour_ref, counts_ref, heat_hbm, cond_hbm, start_hbm, proj_ref,
    out_ref, rms_ref,
    va, vb, heat, cond, inv, pack, got, hedge, hproj, trace, seen, table, idx, ex, eh, ei,
    part, parts,
    load_sem, e_send, e_recv, h_send, h_recv, p_send, p_recv, s_send, s_recv,
):
    layers, width = start_hbm.shape
    tiles = width // LANES
    halo = tiles
    ntiles = tiles + 1
    blocks_of_rows = layers // LANES
    b = lax.axis_index("blk")
    k = lax.axis_index("in")
    before, after = lax.rem(b + nblk - 1, nblk), lax.rem(b + 1, nblk)
    lower, upper = lax.rem(k + nin - 1, nin), lax.rem(k + 1, nin)
    has_lower, has_upper = k > 0, k < nin - 1
    top = SUB
    last = SUB + layers - 1

    loads = []
    for a, (src, dst, off) in enumerate(
        ((start_hbm, va, SUB), (heat_hbm, heat, 0), (cond_hbm, cond, 0))
    ):
        for t in range(tiles):
            c = pltpu.make_async_copy(
                src.at[:, pl.ds(t * LANES, LANES)],
                dst.at[t, pl.ds(off, layers)],
                load_sem.at[a, t],
            )
            c.start()
            loads.append(c)

    barrier = pltpu.get_barrier_semaphore()

    def greet(i, _):
        for block in (before, after):
            pl.semaphore_signal(barrier, inc=1, device_id=(block, i), device_id_type=MESH)
        return 0

    def greet_own(i, _):
        pl.semaphore_signal(
            barrier, inc=1, device_id=(b, lax.rem(k + i, nin)), device_id_type=MESH
        )
        return 0

    lax.fori_loop(0, nin, greet, 0)
    lax.fori_loop(1, nin, greet_own, 0)

    zeros = jnp.zeros((SUB, LANES), F32)
    for v in (va, vb):
        for t in range(ntiles):
            v[t, pl.ds(0, SUB)] = zeros
            v[t, pl.ds(SUB + layers, SUB)] = zeros

    pl.semaphore_wait(barrier, 3 * nin - 1)

    def exchange(stage):
        def send(i, _):
            for side, block in ((0, after), (1, before)):
                pltpu.make_async_remote_copy(
                    src_ref=trace.at[stage, side],
                    dst_ref=seen.at[stage, side, k],
                    send_sem=e_send.at[stage],
                    recv_sem=e_recv.at[stage, side],
                    device_id=(block, i),
                    device_id_type=MESH,
                ).start()
            return 0

        lax.fori_loop(0, nin, send, 0)

    def bytes_of(ref, sem):
        pltpu.make_async_copy(ref, ref, sem).wait()

    for c in loads[:tiles]:
        c.wait()
    for t in range(tiles):
        trace[0, 0, pl.ds(t, 1)] = va[t, pl.ds(last, 1)]
        trace[0, 1, pl.ds(t, 1)] = va[t, pl.ds(top, 1)]
    exchange(0)

    def edge_sends(a, ref, off):
        for d, (peer, t) in enumerate(((lower, 0), (upper, tiles - 1))):
            for side, row in ((0, 0), (1, layers - WINDOW)):
                pltpu.make_async_remote_copy(
                    src_ref=ref.at[t, pl.ds(off + row, WINDOW)],
                    dst_ref=hedge.at[d, a, side],
                    send_sem=h_send.at[0],
                    recv_sem=h_recv.at[0, d],
                    device_id=(b, peer),
                    device_id_type=MESH,
                ).start()

    edge_sends(0, va, SUB)
    for d, (peer, t) in enumerate(((lower, 0), (upper, tiles - 1))):
        pltpu.make_async_remote_copy(
            src_ref=proj_ref.at[:, pl.ds(t * LANES, LANES)],
            dst_ref=hproj.at[d],
            send_sem=h_send.at[1],
            recv_sem=h_recv.at[1, d],
            device_id=(b, peer),
            device_id_type=MESH,
        ).start()
    for c in loads[tiles:]:
        c.wait()
    edge_sends(1, heat, 0)
    edge_sends(2, cond, 0)

    lane_block = lax.broadcasted_iota(jnp.int32, (LANES, LANES), 1)

    def packing(i, _):
        at = pl.multiple_of(i * LANES, LANES)
        rows = pl.ds(at, LANES)
        s_rows = pl.ds(pl.multiple_of(at + SUB, SUB), LANES)
        s0, s1 = va[0, s_rows], va[tiles - 1, s_rows]
        h0, h1 = heat[0, rows], heat[tiles - 1, rows]
        c0, c1 = cond[0, rows], cond[tiles - 1, rows]
        x = pltpu.roll(c1, 64, 1)
        x = jnp.where(lane_block < 56, pltpu.roll(h1, 56, 1), x)
        x = jnp.where(lane_block < 48, pltpu.roll(s1, 48, 1), x)
        x = jnp.where(lane_block < 32, pltpu.roll(c0, 24, 1), x)
        x = jnp.where(lane_block < 24, pltpu.roll(h0, 16, 1), x)
        x = jnp.where(lane_block < 16, s0, x)
        y = x.T
        pack[0, :, rows] = y[:STRIP]
        pack[1, :, rows] = y[STRIP : 2 * STRIP]
        return 0

    lax.fori_loop(0, blocks_of_rows, packing, 0)
    strips = []
    for d, peer in enumerate((lower, upper)):
        c = pltpu.make_async_remote_copy(
            src_ref=pack.at[d],
            dst_ref=got.at[d],
            send_sem=p_send.at[d],
            recv_sem=p_recv.at[d],
            device_id=(b, peer),
            device_id_type=MESH,
        )
        c.start()
        strips.append(c)

    def inverses(i, _):
        rows = pl.ds(pl.multiple_of(i * CHUNK, CHUNK), CHUNK)
        for t in range(tiles):
            inv[t, rows] = 1.0 / (4.0 + cond[t, rows])
        return 0

    lax.fori_loop(0, layers // CHUNK, inverses, 0)

    lane_w = lax.broadcasted_iota(jnp.int32, (WINDOW, LANES), 1)
    row_w = lax.broadcasted_iota(jnp.int32, (WINDOW, LANES), 0)
    near_upper = (lane_w < 16) & has_upper
    near_lower = (lane_w >= 112) & has_lower
    for d in range(2):
        bytes_of(hedge.at[d], h_recv.at[0, d])
        bytes_of(hproj.at[d], h_recv.at[1, d])
    bytes_of(hedge, h_send.at[0])
    bytes_of(hproj, h_send.at[1])
    for side, row in ((0, 0), (1, layers - WINDOW)):
        for t in range(tiles):
            ex[side, t] = va[t, pl.ds(SUB + row, WINDOW)]
            eh[side, t] = heat[t, pl.ds(row, WINDOW)]
            ei[side, t] = inv[t, pl.ds(row, WINDOW)]

        def joined(a, f):
            r, l = f(hedge[0, a, side]), f(hedge[1, a, side])
            return jnp.where(near_upper, r, jnp.where(near_lower, l, 0.0))

        ex[side, halo] = joined(0, lambda x: x)
        eh[side, halo] = joined(1, lambda x: x)
        ei[side, halo] = joined(2, lambda x: 1.0 / (4.0 + x))

    lane_row = lax.broadcasted_iota(jnp.int32, (1, LANES), 1)
    for side in range(2):
        for t in range(tiles):
            idx[side, pl.ds(t, 1)] = proj_ref[pl.ds(side, 1), pl.ds(t * LANES, LANES)]
        idx[side, pl.ds(halo, 1)] = jnp.where(
            lane_row < 64, hproj[0, pl.ds(side, 1)], hproj[1, pl.ds(side, 1)]
        )
    sub_iota = lax.broadcasted_iota(jnp.int32, (SUB, LANES), 0)
    exists = (b > 0, b < nblk - 1)

    def ghosts(stage, side, count):
        bytes_of(seen.at[stage, side], e_recv.at[stage, side])
        for i in range(nin):
            table[pl.ds(i * tiles, tiles)] = seen[stage, side, i]
        limit = jnp.where(exists[side], counts_ref[0, side], 0)
        result = []
        for t in range(count):
            at = idx[side, pl.ds(t, 1)]
            low = jnp.broadcast_to(at & (LANES - 1), (SUB, LANES))
            high = jnp.broadcast_to(at >> 7, (SUB, LANES))
            total = jnp.zeros((SUB, LANES), F32)
            for g in range(nin * tiles // SUB):
                picked = jnp.take_along_axis(
                    table[pl.ds(g * SUB, SUB)], low, axis=1, mode="promise_in_bounds"
                )
                total = jnp.where(high == sub_iota + g * SUB, picked, total)
            row = jnp.sum(total, axis=0, keepdims=True)
            if t == halo:
                place = jnp.where(lane_row < 64, k * width + width, k * width - LANES) + lane_row
            else:
                place = k * width + t * LANES + lane_row
            result.append(jnp.where(place < limit, row, 0.0))
        return result

    def edge_stage(stage):
        sweep, colour = stage // 2, stage % 2
        mine = colour_ref[sweep, 0] == colour
        for side in range(2):
            g = ghosts(stage, side, ntiles)
            x = [ex[side, t] for t in range(ntiles)]
            old = x
            for _ in range(INNER):
                left, right = shift_lanes(x, lane_w)
                new = []
                for t in range(ntiles):
                    up = pltpu.roll(x[t], 1, 0)
                    down = pltpu.roll(x[t], WINDOW - 1, 0)
                    if side == 0:
                        up = jnp.where(row_w == 0, g[t], up)
                    else:
                        down = jnp.where(row_w == WINDOW - 1, g[t], down)
                    near = up + down + left[t] + right[t]
                    new.append((eh[side, t] + near) * ei[side, t])
                x = new
            for t in range(ntiles):
                y = jnp.where(mine, x[t], old[t])
                ex[side, t] = y
                if t < tiles:
                    if side == 0:
                        trace[stage + 1, 1, pl.ds(t, 1)] = y[:1]
                    else:
                        trace[stage + 1, 0, pl.ds(t, 1)] = y[WINDOW - 1 :]
        exchange(stage + 1)

    edge_stage(0)

    for c in strips:
        c.wait()

    def unpacking(i, _):
        at = pl.multiple_of(i * LANES, LANES)
        rows = pl.ds(at, LANES)
        x = jnp.concatenate(
            [got[0, :, rows], got[1, :, rows], jnp.zeros((LANES - 2 * STRIP, LANES), F32)], 0
        )
        z = x.T
        up16 = (lane_block < 16) & has_upper
        lo16 = (lane_block >= 112) & has_lower
        up8 = (lane_block < 8) & has_upper
        lo8 = (lane_block >= 120) & has_lower
        va[halo, pl.ds(pl.multiple_of(at + SUB, SUB), LANES)] = jnp.where(
            up16, z, jnp.where(lo16, pltpu.roll(z, 80, 1), 0.0)
        )
        heat[halo, rows] = jnp.where(
            up8, pltpu.roll(z, 112, 1), jnp.where(lo8, pltpu.roll(z, 72, 1), 0.0)
        )
        c = jnp.where(up8, pltpu.roll(z, 104, 1), pltpu.roll(z, 64, 1))
        inv[halo, rows] = jnp.where(up8 | lo8, 1.0 / (4.0 + c), 0.0)
        return 0

    lax.fori_loop(0, blocks_of_rows, unpacking, 0)

    lane_c = lax.broadcasted_iota(jnp.int32, (CHUNK, LANES), 1)

    def step(old, new):
        def body(i, _):
            at = pl.multiple_of(i * CHUNK, CHUNK)
            rows = pl.ds(at, CHUNK)
            mid = pl.ds(pl.multiple_of(at + SUB, SUB), CHUNK)
            x = [old[t, mid] for t in range(ntiles)]
            left, right = shift_lanes(x, lane_c)
            for t in range(ntiles):
                up = old[t, pl.ds(at + SUB - 1, CHUNK)]
                down = old[t, pl.ds(at + SUB + 1, CHUNK)]
                near = up + down + left[t] + right[t]
                new[t, mid] = (heat[t, rows] + near) * inv[t, rows]
            return 0

        lax.fori_loop(0, layers // CHUNK, body, 0)

    for stage in range(1, 2 * SWEEPS):
        step(va, vb)
        step(vb, va)
        edge_stage(stage)
    step(va, vb)
    step(vb, va)

    for side, row, off in ((0, 0, 0), (1, layers - SUB, WINDOW - SUB)):
        for t in range(ntiles):
            va[t, pl.ds(SUB + row, SUB)] = ex[side, t, pl.ds(off, SUB)]

    def misfit(row, size, lane, ghost=None):
        rows = pl.ds(row, size)
        mid = pl.ds(row + SUB, size)
        x = [va[t, mid] for t in range(ntiles)]
        left, right = shift_lanes(x, lane)
        total = None
        for t in range(tiles):
            out_ref[rows, pl.ds(t * LANES, LANES)] = x[t]
            up = va[t, pl.ds(row + SUB - 1, size)]
            down = va[t, pl.ds(row + SUB + 1, size)]
            if ghost is not None:
                side, g = ghost
                if side == 0:
                    up = jnp.where(sub_iota == 0, g[t], up)
                else:
                    down = jnp.where(sub_iota == SUB - 1, g[t], down)
            near = up + down + left[t] + right[t]
            r = heat[t, rows] - ((4.0 + cond[t, rows]) * x[t] - near)
            r = r * r
            total = r if total is None else total + r
        return jnp.sum(total.reshape(size // SUB, SUB, LANES), axis=0)

    size = SUB * 10
    lane_m = lax.broadcasted_iota(jnp.int32, (size, LANES), 1)
    lane_s = lax.broadcasted_iota(jnp.int32, (SUB, LANES), 1)

    def residual(i, total):
        return total + misfit(pl.multiple_of(i * size + SUB, SUB), size, lane_m)

    total = lax.fori_loop(0, (layers - 2 * SUB) // size, residual, jnp.zeros((SUB, LANES), F32))
    rest = SUB + (layers - 2 * SUB) // size * size
    while rest < layers - SUB:
        total = total + misfit(rest, SUB, lane_s)
        rest += SUB
    final = 2 * SWEEPS
    total = total + misfit(0, SUB, lane_s, (0, ghosts(final, 0, tiles)))
    total = total + misfit(layers - SUB, SUB, lane_s, (1, ghosts(final, 1, tiles)))

    mine = jnp.sum(total, axis=0, keepdims=True)
    part[...] = mine

    def share(i, _):
        pltpu.make_async_remote_copy(
            src_ref=part,
            dst_ref=parts.at[k],
            send_sem=s_send,
            recv_sem=s_recv,
            device_id=(b, lax.rem(k + i, nin)),
            device_id_type=MESH,
        ).start()
        return 0

    lax.fori_loop(1, nin, share, 0)
    for stage in range(2 * SWEEPS + 1):
        bytes_of(seen.at[stage], e_send.at[stage])
    parts[k] = mine
    bytes_of(parts.at[pl.ds(0, nin - 1)], s_recv)
    bytes_of(parts.at[pl.ds(0, nin - 1)], s_send)
    whole = parts[0]
    for i in range(1, nin):
        whole = whole + parts[i]
    whole = jnp.sum(whole, axis=1, keepdims=True)
    rms = jnp.sqrt(jnp.broadcast_to(whole, (SUB, LANES)) / (layers * width * nin) + 1e-6)
    rms_ref[0] = rms[0, 0]


def solution(mesh):
    nblk, nin = mesh.shape["blk"], mesh.shape["in"]

    def per_device(heat_source, conductance, start_field, colour_map, projection, face_counts):
        layers, width = start_field.shape
        tiles = width // LANES
        n = tiles + 1
        stages = 2 * SWEEPS + 1
        vmem, smem = pltpu.VMEM, pltpu.SMEM
        dma = pltpu.SemaphoreType.DMA
        field, rms = pl.pallas_call(
            functools.partial(kernel, nblk, nin),
            out_shape=(
                jax.ShapeDtypeStruct((layers, width), F32),
                jax.ShapeDtypeStruct((1,), F32),
            ),
            in_specs=[
                pl.BlockSpec(memory_space=smem),
                pl.BlockSpec(memory_space=smem),
                pl.BlockSpec(memory_space=pl.ANY),
                pl.BlockSpec(memory_space=pl.ANY),
                pl.BlockSpec(memory_space=pl.ANY),
                pl.BlockSpec(memory_space=vmem),
            ],
            out_specs=(pl.BlockSpec(memory_space=vmem), pl.BlockSpec(memory_space=smem)),
            scratch_shapes=[
                vmem((n, layers + 2 * SUB, LANES), F32),
                vmem((n, layers + 2 * SUB, LANES), F32),
                vmem((n, layers, LANES), F32),
                vmem((tiles, layers, LANES), F32),
                vmem((n, layers, LANES), F32),
                vmem((2, STRIP, layers), F32),
                vmem((2, STRIP, layers), F32),
                vmem((2, 3, 2, WINDOW, LANES), F32),
                vmem((2, 2, LANES), jnp.int32),
                vmem((stages, 2, tiles, LANES), F32),
                vmem((stages, 2, nin, tiles, LANES), F32),
                vmem((nin * tiles, LANES), F32),
                vmem((2, SUB, LANES), jnp.int32),
                vmem((2, n, WINDOW, LANES), F32),
                vmem((2, n, WINDOW, LANES), F32),
                vmem((2, n, WINDOW, LANES), F32),
                vmem((1, LANES), F32),
                vmem((nin, 1, LANES), F32),
                dma((3, tiles)),
                dma((stages,)),
                dma((stages, 2)),
                dma((2,)),
                dma((2, 2)),
                dma((2,)),
                dma((2,)),
                dma,
                dma,
            ],
            compiler_params=pltpu.CompilerParams(
                collective_id=0, has_side_effects=True, vmem_limit_bytes=40 * 1024 * 1024
            ),
        )(
            colour_map, face_counts, heat_source, conductance, start_field,
            projection.reshape(projection.shape[1:]),
        )
        return field, rms

    placed = (
        P("blk", "in"),
        P("blk", "in"),
        P("blk", "in"),
        P(None, "blk"),
        P("blk", None, "in"),
        P("blk", None),
    )
    return jax.shard_map(
        per_device,
        mesh=mesh,
        in_specs=placed,
        out_specs=(P("blk", "in"), P("blk")),
        check_vma=False,
    )
```

profile of v0, /device:TPU:0, one launch (start us, length us, event | category | flops | bytes accessed | tf_op | source)
XLA Modules:
  0.0 63.2 jit_solution(2480056926392574273)
XLA Ops:
  0.6 0.7 %copy.8.colour_ref = s32[2,1]{1,0:T(2,128)S(1)} copy(s32[2,1]{0,1:T(1,128)} %param.9) | data formatting | bytes 16 | tf_op args[3]
  1.4 0.0 copy-start
  1.4 1.4 %copy-done = f32[1536,256]{1,0:T(8,128)S(1)} copy-done((f32[1536,256]{1,0:T(8,128)S(1)}, f32[1536,256]{1,0:T(8,128)}, u32[]{:S(2)}) %copy-start) | copy-done | bytes 1572888
  2.8 0.0 copy-start.1
  2.8 1.4 %copy-done.1 = f32[1536,256]{1,0:T(8,128)S(1)} copy-done((f32[1536,256]{1,0:T(8,128)S(1)}, f32[1536,256]{1,0:T(8,128)}, u32[]{:S(2)}) %copy-start.1) | copy-done | bytes 1572888
  4.2 0.0 copy-start.2
  4.2 1.4 %copy-done.2 = f32[1536,256]{1,0:T(8,128)S(1)} copy-done((f32[1536,256]{1,0:T(8,128)S(1)}, f32[1536,256]{1,0:T(8,128)}, u32[]{:S(2)}) %copy-start.2) | copy-done | bytes 1572888
  5.6 0.0 copy-start.3
  5.6 0.7 %copy-done.3 = s32[1,2,256]{2,1,0:T(2,128)S(1)} copy-done((s32[1,2,256]{2,1,0:T(2,128)S(1)}, s32[1,2,256]{2,1,0:T(2,128)}, u32[]{:S(2)}) %copy-start.3) | copy-done | bytes 2072
  6.3 0.0 copy-start.4
  6.3 0.7 %copy-done.4 = s32[1,2]{1,0:T(1,128)S(1)} copy-done((s32[1,2]{1,0:T(1,128)S(1)}, s32[1,2]{1,0:T(1,128)}, u32[]{:S(2)}) %copy-start.4) | copy-done | bytes 32
  6.9 53.5 %shard_map.77 = (f32[1536,256]{1,0:T(8,128)S(1)}, f32[1]{0:T(128)}) custom-call(s32[2,1]{1,0:T(2,128)S(1)} %copy.8.colour_ref, s32[1,2]{1,0:T(1,128)S(1)} %copy-done.4, f32[1536,256]{1,0:T(8,128)S(1)} %copy-done, f32[1536,256]{1,0:T(8,128)S(1)} %copy-done.1, f32[1536,256]{1,0:T(8,128)S(1)} %copy-done.2, s32[2,256]{1,0:T(2,128)S(1)} %bitcast.1), custom_call_target="tpu_custom_call" | custom-call | tf_op jit(solution)/shard_map/pallas_call | solution.py:401
  60.4 1.1 %copy.11 = f32[1536,256]{1,0:T(8,128)} copy(f32[1536,256]{1,0:T(8,128)S(1)} %get-tuple-element.4) | data formatting | bytes 3145728
Async XLA Ops:
  1.4 1.4 %copy-start = (f32[1536,256]{1,0:T(8,128)S(1)}, f32[1536,256]{1,0:T(8,128)}, u32[]{:S(2)}) copy-start(f32[1536,256]{1,0:T(8,128)} %heat_hbm.1) | copy-start | bytes 4718596
  2.8 1.4 %copy-start.1 = (f32[1536,256]{1,0:T(8,128)S(1)}, f32[1536,256]{1,0:T(8,128)}, u32[]{:S(2)}) copy-start(f32[1536,256]{1,0:T(8,128)} %cond_hbm.1) | copy-start | bytes 4718596
  4.2 1.4 %copy-start.2 = (f32[1536,256]{1,0:T(8,128)S(1)}, f32[1536,256]{1,0:T(8,128)}, u32[]{:S(2)}) copy-start(f32[1536,256]{1,0:T(8,128)} %start_hbm.1) | copy-start | bytes 4718596
  5.6 0.7 %copy-start.3 = (s32[1,2,256]{2,1,0:T(2,128)S(1)}, s32[1,2,256]{2,1,0:T(2,128)}, u32[]{:S(2)}) copy-start(s32[1,2,256]{2,1,0:T(2,128)} %param.10) | copy-start | bytes 6148
  6.3 0.7 %copy-start.4 = (s32[1,2]{1,0:T(1,128)S(1)}, s32[1,2]{1,0:T(1,128)}, u32[]{:S(2)}) copy-start(s32[1,2]{1,0:T(1,128)} %counts_ref.1) | copy-start | bytes 28
where the time goes:
time: 63.5 us; the launch traced here: 63.2 us
  Pallas kernels  53.5 us (84%)
  local copies, waits for them, and re-layouts  7.45 us (12%)
  between operations  2.33 us (4%)
    pallas_call x1, Pallas kernels, per_device(): pl.pallas_call(functools.partial(kernel, nblk, nin), out_shape=(jax.Shape...  53.5 us
    unnamed x12, local copies, waits for them, and re-layouts  7.45 us

commit v1 on v0

--- a/solution.py
+++ b/solution.py
@@ -13,7 +13,7 @@
 SUB = 8
 WINDOW = 16
 STRIP = 32
-CHUNK = 64
+CHUNK = 256
 MESH = pl.DeviceIdType.MESH
 F32 = jnp.float32
 
@@ -28,11 +28,12 @@
 
 
 def kernel(
-    nblk, nin, colour_ref, counts_ref, heat_hbm, cond_hbm, start_hbm, proj_ref,
+    nblk, nin, colour_hbm, counts_hbm, heat_hbm, cond_hbm, start_hbm, proj_hbm,
     out_ref, rms_ref,
+    colour_ref, counts_ref, proj_ref,
     va, vb, heat, cond, inv, pack, got, hedge, hproj, trace, seen, table, idx, ex, eh, ei,
     part, parts,
-    load_sem, e_send, e_recv, h_send, h_recv, p_send, p_recv, s_send, s_recv,
+    load_sem, small_sem, e_send, e_recv, h_send, h_recv, p_send, p_recv, s_send, s_recv,
 ):
     layers, width = start_hbm.shape
     tiles = width // LANES
@@ -44,6 +45,7 @@
     before, after = lax.rem(b + nblk - 1, nblk), lax.rem(b + 1, nblk)
     lower, upper = lax.rem(k + nin - 1, nin), lax.rem(k + 1, nin)
     has_lower, has_upper = k > 0, k < nin - 1
+    has_before, has_after = b > 0, b < nblk - 1
     top = SUB
     last = SUB + layers - 1
 
@@ -59,6 +61,13 @@
             )
             c.start()
             loads.append(c)
+    small = []
+    for i, (src, dst) in enumerate(
+        ((proj_hbm, proj_ref), (colour_hbm, colour_ref), (counts_hbm, counts_ref))
+    ):
+        c = pltpu.make_async_copy(src, dst, small_sem.at[i])
+        c.start()
+        small.append(c)
 
     barrier = pltpu.get_barrier_semaphore()
 
@@ -82,59 +91,8 @@
             v[t, pl.ds(0, SUB)] = zeros
             v[t, pl.ds(SUB + layers, SUB)] = zeros
 
-    pl.semaphore_wait(barrier, 3 * nin - 1)
-
-    def exchange(stage):
-        def send(i, _):
-            for side, block in ((0, after), (1, before)):
-                pltpu.make_async_remote_copy(
-                    src_ref=trace.at[stage, side],
-                    dst_ref=seen.at[stage, side, k],
-                    send_sem=e_send.at[stage],
-                    recv_sem=e_recv.at[stage, side],
-                    device_id=(block, i),
-                    device_id_type=MESH,
-                ).start()
-            return 0
-
-        lax.fori_loop(0, nin, send, 0)
-
-    def bytes_of(ref, sem):
-        pltpu.make_async_copy(ref, ref, sem).wait()
-
-    for c in loads[:tiles]:
+    for c in loads:
         c.wait()
-    for t in range(tiles):
-        trace[0, 0, pl.ds(t, 1)] = va[t, pl.ds(last, 1)]
-        trace[0, 1, pl.ds(t, 1)] = va[t, pl.ds(top, 1)]
-    exchange(0)
-
-    def edge_sends(a, ref, off):
-        for d, (peer, t) in enumerate(((lower, 0), (upper, tiles - 1))):
-            for side, row in ((0, 0), (1, layers - WINDOW)):
-                pltpu.make_async_remote_copy(
-                    src_ref=ref.at[t, pl.ds(off + row, WINDOW)],
-                    dst_ref=hedge.at[d, a, side],
-                    send_sem=h_send.at[0],
-                    recv_sem=h_recv.at[0, d],
-                    device_id=(b, peer),
-                    device_id_type=MESH,
-                ).start()
-
-    edge_sends(0, va, SUB)
-    for d, (peer, t) in enumerate(((lower, 0), (upper, tiles - 1))):
-        pltpu.make_async_remote_copy(
-            src_ref=proj_ref.at[:, pl.ds(t * LANES, LANES)],
-            dst_ref=hproj.at[d],
-            send_sem=h_send.at[1],
-            recv_sem=h_recv.at[1, d],
-            device_id=(b, peer),
-            device_id_type=MESH,
-        ).start()
-    for c in loads[tiles:]:
-        c.wait()
-    edge_sends(1, heat, 0)
-    edge_sends(2, cond, 0)
 
     lane_block = lax.broadcasted_iota(jnp.int32, (LANES, LANES), 1)
 
@@ -157,9 +115,48 @@
         return 0
 
     lax.fori_loop(0, blocks_of_rows, packing, 0)
-    strips = []
-    for d, peer in enumerate((lower, upper)):
-        c = pltpu.make_async_remote_copy(
+    def inverses(i, _):
+        rows = pl.ds(pl.multiple_of(i * CHUNK, CHUNK), CHUNK)
+        for t in range(tiles):
+            inv[t, rows] = 1.0 / (4.0 + cond[t, rows])
+        return 0
+
+    lax.fori_loop(0, layers // CHUNK, inverses, 0)
+
+    pl.semaphore_wait(barrier, 3 * nin - 1)
+
+    def exchange(stage):
+        for side, block, there in ((0, after, has_after), (1, before, has_before)):
+
+            @pl.when(there)
+            def _():
+                def send(i, _):
+                    pltpu.make_async_remote_copy(
+                        src_ref=trace.at[stage, side],
+                        dst_ref=seen.at[stage, side, k],
+                        send_sem=e_send.at[stage, side],
+                        recv_sem=e_recv.at[stage, side],
+                        device_id=(block, i),
+                        device_id_type=MESH,
+                    ).start()
+                    return 0
+
+                lax.fori_loop(0, nin, send, 0)
+
+    def bytes_of(ref, sem):
+        pltpu.make_async_copy(ref, ref, sem).wait()
+
+    for t in range(tiles):
+        trace[0, 0, pl.ds(t, 1)] = va[t, pl.ds(last, 1)]
+        trace[0, 1, pl.ds(t, 1)] = va[t, pl.ds(top, 1)]
+    exchange(0)
+
+    for c in small:
+        c.wait()
+    sides = ((lower, 0, has_lower), (upper, tiles - 1, has_upper))
+
+    def strip(d, peer):
+        return pltpu.make_async_remote_copy(
             src_ref=pack.at[d],
             dst_ref=got.at[d],
             send_sem=p_send.at[d],
@@ -167,26 +164,42 @@
             device_id=(b, peer),
             device_id_type=MESH,
         )
-        c.start()
-        strips.append(c)
-
-    def inverses(i, _):
-        rows = pl.ds(pl.multiple_of(i * CHUNK, CHUNK), CHUNK)
-        for t in range(tiles):
-            inv[t, rows] = 1.0 / (4.0 + cond[t, rows])
-        return 0
-
-    lax.fori_loop(0, layers // CHUNK, inverses, 0)
+
+    for d, (peer, t, there) in enumerate(sides):
+
+        @pl.when(there)
+        def _():
+            for a, (ref, off) in enumerate(((va, SUB), (heat, 0), (cond, 0))):
+                for side, row in ((0, 0), (1, layers - WINDOW)):
+                    pltpu.make_async_remote_copy(
+                        src_ref=ref.at[t, pl.ds(off + row, WINDOW)],
+                        dst_ref=hedge.at[d, a, side],
+                        send_sem=h_send.at[0, d],
+                        recv_sem=h_recv.at[0, d],
+                        device_id=(b, peer),
+                        device_id_type=MESH,
+                    ).start()
+            pltpu.make_async_remote_copy(
+                src_ref=proj_ref.at[:, pl.ds(t * LANES, LANES)],
+                dst_ref=hproj.at[d],
+                send_sem=h_send.at[1, d],
+                recv_sem=h_recv.at[1, d],
+                device_id=(b, peer),
+                device_id_type=MESH,
+            ).start()
+            strip(d, peer).start()
 
     lane_w = lax.broadcasted_iota(jnp.int32, (WINDOW, LANES), 1)
     row_w = lax.broadcasted_iota(jnp.int32, (WINDOW, LANES), 0)
     near_upper = (lane_w < 16) & has_upper
     near_lower = (lane_w >= 112) & has_lower
-    for d in range(2):
-        bytes_of(hedge.at[d], h_recv.at[0, d])
-        bytes_of(hproj.at[d], h_recv.at[1, d])
-    bytes_of(hedge, h_send.at[0])
-    bytes_of(hproj, h_send.at[1])
+    for d, there in ((0, has_upper), (1, has_lower)):
+
+        @pl.when(there)
+        def _():
+            bytes_of(hedge.at[d], h_recv.at[0, d])
+            bytes_of(hproj.at[d], h_recv.at[1, d])
+
     for side, row in ((0, 0), (1, layers - WINDOW)):
         for t in range(tiles):
             ex[side, t] = va[t, pl.ds(SUB + row, WINDOW)]
@@ -209,10 +222,13 @@
             lane_row < 64, hproj[0, pl.ds(side, 1)], hproj[1, pl.ds(side, 1)]
         )
     sub_iota = lax.broadcasted_iota(jnp.int32, (SUB, LANES), 0)
-    exists = (b > 0, b < nblk - 1)
+    exists = (has_before, has_after)
 
     def ghosts(stage, side, count):
-        bytes_of(seen.at[stage, side], e_recv.at[stage, side])
+        @pl.when(exists[side])
+        def _():
+            bytes_of(seen.at[stage, side], e_recv.at[stage, side])
+
         for i in range(nin):
             table[pl.ds(i * tiles, tiles)] = seen[stage, side, i]
         limit = jnp.where(exists[side], counts_ref[0, side], 0)
@@ -237,7 +253,7 @@
 
     def edge_stage(stage):
         sweep, colour = stage // 2, stage % 2
-        mine = colour_ref[sweep, 0] == colour
+        mine = colour_ref[0, sweep] == colour
         for side in range(2):
             g = ghosts(stage, side, ntiles)
             x = [ex[side, t] for t in range(ntiles)]
@@ -267,8 +283,19 @@
 
     edge_stage(0)
 
-    for c in strips:
-        c.wait()
+    for d, there in ((0, has_upper), (1, has_lower)):
+
+        @pl.when(there)
+        def _():
+            strip(d, lower).wait_recv()
+
+    for d, (peer, t, there) in enumerate(sides):
+
+        @pl.when(there)
+        def _():
+            bytes_of(hedge.at[d], h_send.at[0, d])
+            bytes_of(hproj.at[d], h_send.at[1, d])
+
 
     def unpacking(i, _):
         at = pl.multiple_of(i * LANES, LANES)
@@ -375,8 +402,19 @@
         return 0
 
     lax.fori_loop(1, nin, share, 0)
+    for d, (peer, t, there) in enumerate(sides):
+
+        @pl.when(there)
+        def _():
+            strip(d, peer).wait_send()
+
     for stage in range(2 * SWEEPS + 1):
-        bytes_of(seen.at[stage], e_send.at[stage])
+        for side, there in ((0, has_after), (1, has_before)):
+
+            @pl.when(there)
+            def _():
+                bytes_of(seen.at[stage, side], e_send.at[stage, side])
+
     parts[k] = mine
     bytes_of(parts.at[pl.ds(0, nin - 1)], s_recv)
     bytes_of(parts.at[pl.ds(0, nin - 1)], s_send)
@@ -404,16 +442,12 @@
                 jax.ShapeDtypeStruct((layers, width), F32),
                 jax.ShapeDtypeStruct((1,), F32),
             ),
-            in_specs=[
-                pl.BlockSpec(memory_space=smem),
-                pl.BlockSpec(memory_space=smem),
-                pl.BlockSpec(memory_space=pl.ANY),
-                pl.BlockSpec(memory_space=pl.ANY),
-                pl.BlockSpec(memory_space=pl.ANY),
-                pl.BlockSpec(memory_space=vmem),
-            ],
+            in_specs=[pl.BlockSpec(memory_space=pltpu.HBM)] * 6,
             out_specs=(pl.BlockSpec(memory_space=vmem), pl.BlockSpec(memory_space=smem)),
             scratch_shapes=[
+                smem((1, SWEEPS), jnp.int32),
+                smem((1, 2), jnp.int32),
+                vmem((2, width), jnp.int32),
                 vmem((n, layers + 2 * SUB, LANES), F32),
                 vmem((n, layers + 2 * SUB, LANES), F32),
                 vmem((n, layers, LANES), F32),
@@ -433,9 +467,10 @@
                 vmem((1, LANES), F32),
                 vmem((nin, 1, LANES), F32),
                 dma((3, tiles)),
-                dma((stages,)),
+                dma((3,)),
                 dma((stages, 2)),
-                dma((2,)),
+                dma((stages, 2)),
+                dma((2, 2)),
                 dma((2, 2)),
                 dma((2,)),
                 dma((2,)),
@@ -443,10 +478,10 @@
                 dma,
             ],
             compiler_params=pltpu.CompilerParams(
-                collective_id=0, has_side_effects=True, vmem_limit_bytes=40 * 1024 * 1024
+                collective_id=0, has_side_effects=True, vmem_limit_bytes=65 * 1000 * 1000
             ),
         )(
-            colour_map, face_counts, heat_source, conductance, start_field,
+            colour_map.T, face_counts, heat_source, conductance, start_field,
             projection.reshape(projection.shape[1:]),
         )
         return field, rms

time: 63.5 us -> 47.4 us (0.75)
  Pallas kernels: 53.5 us -> 42.1 us
  local copies, waits for them, and re-layouts: 7.45 us -> 2.65 us
    pallas_call x1, Pallas kernels: 53.5 us -> 42.1 us  [per_device(): pl.pallas_call(functools.partial(kernel, nblk, nin), out_shape=(jax.Shape...]
    unnamed x12 -> x1, local copies, waits for them, and re-layouts: 7.45 us -> 2.65 us
where the time goes in v1:
time: 47.4 us; the launch traced here: 47.2 us
  Pallas kernels  42.1 us (89%)
  local copies, waits for them, and re-layouts  2.65 us (6%)
  between operations  2.41 us (5%)
    pallas_call x1, Pallas kernels, per_device(): pl.pallas_call(functools.partial(kernel, nblk, nin), out_shape=(jax.Shape...  42.1 us
    unnamed x1, local copies, waits for them, and re-layouts  2.65 us

profile of v1, /device:TPU:0, one launch (start us, length us, event | category | flops | bytes accessed | tf_op | source)
XLA Modules:
  0.0 47.2 jit_solution(17894956319515733291)
XLA Ops:
  0.6 42.1 %shard_map.77 = (f32[1536,256]{1,0:T(8,128)}, f32[1]{0:T(128)}) custom-call(s32[1,2]{1,0:T(1,128)} %bitcast.3, s32[1,2]{1,0:T(1,128)} %counts_hbm.1, f32[1536,256]{1,0:T(8,128)} %heat_hbm.1, f32[1536,256]{1,0:T(8,128)} %cond_hbm.1, f32[1536,256]{1,0:T(8,128)} %start_hbm.1, s32[2,256]{1,0:T(2,128)} %bitcast.2), custom_call_target="tpu_custom_call" | custom-call | tf_op jit(solution)/shard_map/pallas_call | solution.py:439
  42.8 2.7 %copy.10 = f32[1536,256]{1,0:T(8,128)} copy(f32[1536,256]{1,0:T(8,128)} %get-tuple-element.4) | data formatting | bytes 3145728
